TPU v7x, 32 devices: a whole 2x2x4 slice. The times are simulated.
32 devices in a mesh: depth: 8 (over z, y), height: 2 (over core), view: 2 (over x).
Axes of the slice: x: 2, y: 2, z: 4, core: 2. Of those that a mesh axis runs over, the one named last changes fastest.
Arguments:
- camera_feats: bfloat16 [256, 16, 128], P(('depth', 'height', 'view')), may hold values from -6 to 6
- footprint_slot_weights: bfloat16 [8, 128, 128], replicated, may hold values from -0.1875 to 0.1875
- tile_bricks: int32 [256, 8], P(('depth', 'height', 'view')), may hold values from 0 to 1
- tile_rows: int32 [256, 8], P(('depth', 'height', 'view')), may hold values from 0 to 7
- conv_first: bfloat16 [16, 16, 3, 3, 3], replicated, may hold values from -0.3125 to 0.3125
- conv_second: bfloat16 [16, 16, 3, 3, 3], replicated, may hold values from -0.3125 to 0.3125
- conv_third: bfloat16 [16, 16, 3, 3, 3], replicated, may hold values from -0.3125 to 0.3125
- bias_first: float32 [16], replicated, may hold values from -3 to 3
- bias_second: float32 [16], replicated, may hold values from -3 to 3
- out_grad: bfloat16 [16, 16, 16, 128], P(('depth', 'view'), 'height'), may hold values from -6 to 6
Outputs:
- field: bfloat16 [16, 16, 16, 128], P(('depth', 'view'), 'height')
- camera_tile_feature_gradient: float32 [256, 16, 128], P(('depth', 'height', 'view'))
- weight_grads: float32 [3, 16, 16, 3, 3, 3], replicated
- bias_gradient_pair: float32 [2, 16], replicated
All inputs are finite; a program needn't handle non-finite values.
Results may differ from a plain program's by a relative error of at most 0.017.
Values may be sent and summed in bfloat16 or wider, within the bound.
A program may use at most 64 MiB of HBM per device.

v0:
```python
import math

import jax
import jax.numpy as jnp
from jax import lax
from jax.experimental import pallas as pl
from jax.experimental.pallas import tpu as pltpu
from jax.sharding import PartitionSpec as P

MESH = pl.DeviceIdType.MESH
F32 = jnp.float32
BF16 = jnp.bfloat16
DIRS = [(dz, dy) for dz in (-1, 0, 1) for dy in (0, -1, 1) if (dz, dy) != (0, 0)]
LIFT, ACT1, ACT2, OUTG, BACK2, BACK1 = range(6)
BIAS_ROWS = 16


def round_up(value, step):
    return -(-value // step) * step


def silu_grad(values):
    sigma = jax.nn.sigmoid(values)
    return sigma * (1.0 + values * (1.0 - sigma))


def make_kernel(depths, heights, views, tiles, slots, rows_y, channels, width):
    group = heights * views
    wrows = 9 * channels
    srows = 3 * channels
    cells = rows_y * channels
    total_rows = wrows + BIAS_ROWS
    piece = round_up(-(-total_rows // depths), 8)

    def kernel(
        bricks_ref, rows_ref, feats_ref, foot_ref, w_ref, bias_ref, outg_ref,
        field_ref, camera_ref, early_out, late_out,
        vol, part, rsbuf, grid, own_sum, ar_rs, ar_mid,
        halo_send, halo_recv, view_send, view_recv, ar_send, ar_recv,
    ):
        d = lax.axis_index("depth")
        h = lax.axis_index("height")
        v = lax.axis_index("view")
        z = d * views + v
        planes = depths * views

        def exists(dz, dy):
            tests = []
            if dz == -1:
                tests.append(z > 0)
            if dz == 1:
                tests.append(z < planes - 1)
            if dy == -1:
                tests.append(h > 0)
            if dy == 1:
                tests.append(h < heights - 1)
            result = tests[0]
            for test in tests[1:]:
                result = jnp.logical_and(result, test)
            return result

        def neighbour(dz, dy):
            to = z + dz
            return {"depth": lax.div(to, views), "view": lax.rem(to, views), "height": h + dy}

        def halo_slot(index, dz, dy):
            if dy == 0:
                return vol.at[index, 1 - dz, pl.ds(1, rows_y)]
            return vol.at[index, 1 - dz, pl.ds(0 if dy == 1 else rows_y + 1, 1)]

        def halo_source(index, dy):
            base = vol.at[index, 1]
            if dy == 0:
                return base.at[pl.ds(1, rows_y)]
            return base.at[pl.ds(rows_y if dy == 1 else 1, 1)]

        def halo_copy(index, n):
            dz, dy = DIRS[n]
            return pltpu.make_async_remote_copy(
                src_ref=halo_source(index, dy),
                dst_ref=halo_slot(index, dz, dy),
                send_sem=halo_send.at[index, n],
                recv_sem=halo_recv.at[index, n],
                device_id=neighbour(dz, dy),
                device_id_type=MESH,
            )

        def halo_start(index):
            for n, (dz, dy) in enumerate(DIRS):
                @pl.when(exists(dz, dy))
                def _():
                    halo_copy(index, n).start()

        def halo_wait(index):
            for n, (dz, dy) in enumerate(DIRS):
                @pl.when(exists(-dz, -dy))
                def _():
                    halo_copy(index, n).wait_recv()

        def halo_drain(index):
            for n, (dz, dy) in enumerate(DIRS):
                @pl.when(exists(dz, dy))
                def _():
                    halo_copy(index, n).wait_send()

        view_peers = [{"view": lax.rem(v + k, views)} for k in range(1, views)]
        depth_peers = [{"depth": lax.rem(d + k, depths)} for k in range(1, depths)]
        me = h * views + v
        group_peers = []
        for k in range(1, group):
            to = lax.rem(me + k, group)
            group_peers.append((to, {"height": lax.div(to, views), "view": lax.rem(to, views)}))

        barrier = pltpu.get_barrier_semaphore()
        for dz, dy in DIRS:
            @pl.when(exists(dz, dy))
            def _():
                pl.semaphore_signal(barrier, inc=1, device_id=neighbour(dz, dy), device_id_type=MESH)
        for peer in view_peers + depth_peers + [p for _, p in group_peers]:
            pl.semaphore_signal(barrier, inc=1, device_id=peer, device_id_type=MESH)

        for dz, dy in DIRS:
            @pl.when(jnp.logical_not(exists(-dz, -dy)))
            def _():
                for index in range(6):
                    slot = halo_slot(index, dz, dy)
                    slot[...] = jnp.zeros(slot.shape, BF16)
        vol[OUTG, 1, pl.ds(1, rows_y)] = outg_ref[0]

        nrow = views * rows_y
        lane = lax.broadcasted_iota(jnp.int32, (1, tiles * channels), 1)
        row_id = lax.broadcasted_iota(jnp.int32, (nrow * channels, tiles * channels), 0)
        col_id = lax.broadcasted_iota(jnp.int32, (nrow * channels, tiles * channels), 1)
        same_channel = lax.rem(row_id, channels) == lax.rem(col_id, channels)
        target_id = jnp.where(same_channel, lax.div(row_id, channels), -1)
        lane_tile = lax.div(lane, channels)
        feats = feats_ref[...].reshape(tiles * channels, -1)
        partial = jnp.zeros((nrow * channels, width), F32)
        for k in range(slots):
            targets = jnp.zeros(lane.shape, jnp.int32)
            for t in range(tiles):
                targets = jnp.where(lane_tile == t, bricks_ref[t, k] * rows_y + rows_ref[t, k], targets)
            chosen = jnp.where(target_id == targets, 1.0, 0.0).astype(BF16)
            picked = jnp.dot(chosen, feats, preferred_element_type=F32).astype(BF16)
            partial += lax.dot_general(
                picked, foot_ref[k], (((1,), (1,)), ((), ())), preferred_element_type=F32
            )
        part[...] = partial.astype(BF16).reshape(views, rows_y, channels, width)

        count = len(view_peers) + len(depth_peers) + len(group_peers)
        for dz, dy in DIRS:
            count = count + exists(dz, dy).astype(jnp.int32)
        pl.semaphore_wait(barrier, count)

        def part_copy(k):
            to = lax.rem(v + k, views)
            return pltpu.make_async_remote_copy(
                src_ref=part.at[to], dst_ref=rsbuf.at[k],
                send_sem=view_send.at[0, k], recv_sem=view_recv.at[0, k],
                device_id={"view": to}, device_id_type=MESH,
            )

        for k in range(1, views):
            part_copy(k).start()
        halo_start(OUTG)

        def im2col(index):
            columns = []
            for y in range(rows_y):
                columns.append(jnp.concatenate(
                    [vol[index, a, pl.ds(y, 3)].reshape(srows, width) for a in range(3)], axis=0
                ))
            return jnp.concatenate(columns, axis=1)

        def to_rows(wide):
            return jnp.concatenate([wide[:, y * width:(y + 1) * width] for y in range(rows_y)], axis=0)

        def to_wide(tall):
            return jnp.concatenate([tall[y * channels:(y + 1) * channels] for y in range(rows_y)], axis=1)

        x_id = lax.broadcasted_iota(jnp.int32, (cells, width), 1)

        def from_left(values):
            return jnp.where(x_id == 0, 0.0, pltpu.roll(values, 1, 1))

        def from_right(values):
            return jnp.where(x_id == width - 1, 0.0, pltpu.roll(values, width - 1, 1))

        def conv(which, columns):
            taps = jnp.dot(w_ref[which], columns, preferred_element_type=F32)
            low, mid, high = (to_rows(taps[n * channels:(n + 1) * channels]) for n in range(3))
            return from_left(low) + mid + from_right(high)

        def grad_rows(grads):
            exact = grads.astype(F32)
            return [
                to_wide(from_right(exact).astype(BF16)),
                to_wide(grads),
                to_wide(from_left(exact).astype(BF16)),
            ]

        def weight_grad(columns, pieces):
            stacked = jnp.concatenate(pieces, axis=0)
            return lax.dot_general(columns, stacked, (((1,), (1,)), ((), ())), preferred_element_type=F32)

        def blank(rows):
            return jnp.zeros((rows, rows_y * width), BF16)

        def rows_sum(values):
            total = values[0:channels]
            for y in range(1, rows_y):
                total = total + values[y * channels:(y + 1) * channels]
            return total

        def tall_bias(n):
            return jnp.concatenate([bias_ref[n]] * rows_y, axis=0)

        def put(index, values):
            vol[index, 1, pl.ds(1, rows_y)] = values.reshape(rows_y, channels, width)

        outs = (early_out, late_out)

        def ar_a(n, k):
            to = lax.rem(d + k, depths)
            return pltpu.make_async_remote_copy(
                src_ref=own_sum.at[n, pl.ds(pl.multiple_of(to * piece, 8), piece)], dst_ref=ar_rs.at[n, k],
                send_sem=ar_send.at[n, 0, k], recv_sem=ar_recv.at[n, 0, k],
                device_id={"depth": to}, device_id_type=MESH,
            )

        def ar_b(n, k):
            to, peer = group_peers[k - 1]
            return pltpu.make_async_remote_copy(
                src_ref=ar_mid.at[n, me], dst_ref=ar_mid.at[n, me],
                send_sem=ar_send.at[n, 1, k], recv_sem=ar_recv.at[n, 1, k],
                device_id=peer, device_id_type=MESH,
            )

        def ar_b_in(n, k):
            source = lax.rem(me + group - k, group)
            return pltpu.make_async_remote_copy(
                src_ref=ar_mid.at[n, source], dst_ref=ar_mid.at[n, source],
                send_sem=ar_send.at[n, 1, k], recv_sem=ar_recv.at[n, 1, k],
                device_id=group_peers[k - 1][1], device_id_type=MESH,
            )

        def ar_c(n, k, owner):
            to = lax.rem(d + k, depths)
            place = outs[n].at[pl.ds(pl.multiple_of(owner * piece, 8), piece)]
            return pltpu.make_async_remote_copy(
                src_ref=place, dst_ref=place,
                send_sem=ar_send.at[n, 2, k], recv_sem=ar_recv.at[n, 2, k],
                device_id={"depth": to}, device_id_type=MESH,
            )

        def reduce_start(n, values, bias):
            own_sum[n, pl.ds(0, wrows)] = values
            own_sum[n, pl.ds(wrows, BIAS_ROWS)] = bias
            if depths * piece > total_rows:
                rest = depths * piece - total_rows
                own_sum[n, pl.ds(total_rows, rest)] = jnp.zeros((rest, 128), F32)
            for k in range(1, depths):
                ar_a(n, k).start()

        def reduce_middle(n):
            total = own_sum[n, pl.ds(pl.multiple_of(d * piece, 8), piece)]
            for k in range(1, depths):
                ar_a(n, k).wait_recv()
                total = total + ar_rs[n, k]
            ar_mid[n, me] = total
            for k in range(1, group):
                ar_b(n, k).start()

        def reduce_last(n):
            for k in range(1, group):
                ar_b_in(n, k).wait_recv()
            total = ar_mid[n, 0]
            for j in range(1, group):
                total = total + ar_mid[n, j]
            outs[n][pl.ds(pl.multiple_of(d * piece, 8), piece)] = total
            for k in range(1, depths):
                ar_c(n, k, d).start()

        def reduce_end(n):
            for k in range(1, depths):
                ar_c(n, k, lax.rem(d + depths - k, depths)).wait_recv()

        def reduce_drain(n):
            for k in range(1, depths):
                ar_a(n, k).wait_send()
                ar_c(n, k, d).wait_send()
            for k in range(1, group):
                ar_b(n, k).wait_send()

        lifted = part[v].astype(F32)
        for k in range(1, views):
            part_copy(k).wait_recv()
            lifted = lifted + rsbuf[k].astype(F32)
        put(LIFT, lifted.astype(BF16))
        halo_start(LIFT)

        halo_wait(OUTG)
        up_second = conv(3, im2col(OUTG))
        out_pieces = grad_rows(outg_ref[0].reshape(cells, width))

        halo_wait(LIFT)
        pre_first = conv(0, im2col(LIFT)) + tall_bias(0)
        act_first = jax.nn.silu(pre_first).astype(BF16)
        put(ACT1, act_first)
        halo_start(ACT1)
        slope_of_first = silu_grad(pre_first)

        halo_wait(ACT1)
        columns_second = im2col(ACT1)
        pre_second = conv(1, columns_second) + tall_bias(1)
        slope_second = up_second * silu_grad(pre_second)
        back_second = slope_second.astype(BF16)
        put(BACK2, back_second)
        halo_start(BACK2)
        act_second = (jax.nn.silu(pre_second) + act_first.astype(F32)).astype(BF16)
        put(ACT2, act_second)
        halo_start(ACT2)
        early = weight_grad(columns_second, grad_rows(back_second) + [blank(128 - srows)])

        halo_wait(BACK2)
        up_first = up_second + conv(4, im2col(BACK2))
        slope_first = up_first * slope_of_first
        back_first = slope_first.astype(BF16)
        put(BACK1, back_first)
        halo_start(BACK1)
        late = weight_grad(im2col(LIFT), grad_rows(back_first) + [blank(128 - srows)])
        reduce_start(1, late, rows_sum(slope_first))

        halo_wait(ACT2)
        columns_third = im2col(ACT2)
        field = conv(2, columns_third)
        field_ref[0] = field.astype(BF16).reshape(rows_y, channels, width)
        early = early + weight_grad(
            columns_third, [blank(srows)] + out_pieces + [blank(128 - 2 * srows)]
        )
        reduce_start(0, early, rows_sum(slope_second))

        halo_wait(BACK1)
        lift_grad = conv(5, im2col(BACK1)).astype(BF16)
        grid[v] = lift_grad.reshape(rows_y, channels, width)

        def grid_copy(k, place):
            return pltpu.make_async_remote_copy(
                src_ref=grid.at[place], dst_ref=grid.at[place],
                send_sem=view_send.at[1, k], recv_sem=view_recv.at[1, k],
                device_id={"view": lax.rem(v + k, views)}, device_id_type=MESH,
            )

        for k in range(1, views):
            grid_copy(k, v).start()
        reduce_middle(1)
        reduce_middle(0)
        for k in range(1, views):
            grid_copy(k, lax.rem(v + views - k, views)).wait_recv()
        reduce_last(1)
        reduce_last(0)
        camera = jnp.zeros((tiles * channels, width), F32)
        for k in range(slots):
            picked = jnp.concatenate(
                [grid[bricks_ref[t, k], rows_ref[t, k]] for t in range(tiles)], axis=0
            )
            camera += jnp.dot(picked, foot_ref[k], preferred_element_type=F32)
        camera_ref[...] = camera.reshape(tiles, channels, width)
        reduce_end(1)
        reduce_end(0)
        for index in range(6):
            halo_drain(index)
        for k in range(1, views):
            part_copy(k).wait_send()
            grid_copy(k, v).wait_send()
        for n in range(2):
            reduce_drain(n)

    vmem = pl.BlockSpec(memory_space=pltpu.VMEM)
    smem = pl.BlockSpec(memory_space=pltpu.SMEM)
    plane = (rows_y, channels, width)
    return pl.pallas_call(
        kernel,
        out_shape=(
            jax.ShapeDtypeStruct((1,) + plane, BF16),
            jax.ShapeDtypeStruct((tiles, channels, width), F32),
            jax.ShapeDtypeStruct((depths * piece, 128), F32),
            jax.ShapeDtypeStruct((depths * piece, 128), F32),
        ),
        in_specs=[smem, smem] + [vmem] * 5,
        out_specs=(vmem,) * 4,
        scratch_shapes=[
            pltpu.VMEM((6, 3, rows_y + 2, channels, width), BF16),
            pltpu.VMEM((views,) + plane, BF16),
            pltpu.VMEM((views,) + plane, BF16),
            pltpu.VMEM((views,) + plane, BF16),
            pltpu.VMEM((2, depths * piece, 128), F32),
            pltpu.VMEM((2, depths, piece, 128), F32),
            pltpu.VMEM((2, group, piece, 128), F32),
            pltpu.SemaphoreType.DMA((6, len(DIRS))),
            pltpu.SemaphoreType.DMA((6, len(DIRS))),
            pltpu.SemaphoreType.DMA((2, views)),
            pltpu.SemaphoreType.DMA((2, views)),
            pltpu.SemaphoreType.DMA((2, 3, max(depths, group))),
            pltpu.SemaphoreType.DMA((2, 3, max(depths, group))),
        ],
        compiler_params=pltpu.CompilerParams(collective_id=0, has_side_effects=True),
    )


def forward_matrix(weight):
    c = weight.shape[0]
    return jnp.transpose(weight, (4, 0, 2, 3, 1)).reshape(3 * c, 9 * c)


def backward_matrix(weight):
    c = weight.shape[0]
    return jnp.transpose(jnp.flip(weight, (2, 3, 4)), (4, 1, 2, 3, 0)).reshape(3 * c, 9 * c)


def body(
    camera_feats,
    footprint_slot_weights,
    tile_bricks,
    tile_rows,
    conv_first,
    conv_second,
    conv_third,
    bias_first,
    bias_second,
    out_grad,
):
    depths, heights, views = (lax.axis_size(a) for a in ("depth", "height", "view"))
    tiles, channels, _ = camera_feats.shape
    slots, width, _ = footprint_slot_weights.shape
    rows_y = out_grad.shape[1]
    weights = jnp.stack(
        [forward_matrix(w) for w in (conv_first, conv_second, conv_third)]
        + [backward_matrix(w) for w in (conv_third, conv_second, conv_first)]
    )
    biases = jnp.broadcast_to(
        jnp.stack([bias_first, bias_second])[:, :, None], (2, channels, width)
    )
    call = make_kernel(depths, heights, views, tiles, slots, rows_y, channels, width)
    field, camera, early, late = call(
        tile_bricks, tile_rows, camera_feats, footprint_slot_weights, weights, biases, out_grad
    )
    scale = 1.0 / math.sqrt(rows_y * width * depths * heights * views)
    wrows, srows = 9 * channels, 3 * channels
    parts = jnp.stack([late[:wrows, :srows], early[:wrows, :srows], early[:wrows, srows:2 * srows]])
    parts = parts.reshape(3, 3, 3, channels, 3, channels) * scale
    weight_grads = jnp.transpose(parts, (0, 5, 3, 1, 2, 4))
    sums = jnp.stack([late[wrows:wrows + channels], early[wrows:wrows + channels]])
    return field, camera, weight_grads, jnp.sum(sums, axis=2) * scale


def solution(mesh):
    in_specs = (
        P(("depth", "height", "view"), None, None),
        P(),
        P(("depth", "height", "view"), None),
        P(("depth", "height", "view"), None),
        P(),
        P(),
        P(),
        P(),
        P(),
        P(("depth", "view"), "height", None, None),
    )
    out_specs = (
        P(("depth", "view"), "height", None, None),
        P(("depth", "height", "view"), None, None),
        P(),
        P(),
    )
    return jax.shard_map(body, mesh=mesh, in_specs=in_specs, out_specs=out_specs, check_vma=False)
```

profile of v0, /device:TPU:0, one launch (start us, length us, event | category | flops | bytes accessed | tf_op | source)
XLA Modules:
  0.0 53.9 jit_solution(17461515438800565746)
XLA Ops:
  0.7 0.6 %copy-done.7 = f32[16]{0:T(128)S(1)} copy-done((f32[16]{0:T(128)S(1)}, f32[16]{0:T(128)}, u32[]{:S(2)}) %copy-start.7) | copy-done | bytes 88
  1.3 0.7 %broadcast_in_dim.2.bias_ref = f32[2,16,128]{2,1,0:T(8,128)} broadcast(f32[2,16]{1,0:T(2,128)S(1)} %pad_maximum_fusion), dimensions={0,1} | broadcast | bytes 16512 | tf_op jit(solution)/shard_map/broadcast_in_dim | solution.py:441
  2.0 0.9 %reverse_bitcast_fusion = bf16[3,16,3,3,16]{1,4,0,3,2:T(8,128)(2,1)S(1)} fusion(bf16[16,16,3,3,3]{1,0,4,3,2:T(8,128)(2,1)} %param.14), kind=kLoop, calls=%fused_computation.2 | loop fusion | bytes 27648 | tf_op jit(solution)/shard_map/transpose | solution.py:418
  2.9 0.1 copy.28
  3.1 0.1 stack_reshape.23
  3.2 0.8 %copy-done.1 = bf16[16,16,3,3,3]{1,0,4,3,2:T(8,128)(2,1)S(1)} copy-done((bf16[16,16,3,3,3]{1,0,4,3,2:T(8,128)(2,1)S(1)}, bf16[16,16,3,3,3]{1,0,4,3,2:T(8,128)(2,1)}, u32[]{:S(2)}) %copy-start.1) | copy-done | bytes 13848
  4.0 0.1 copy.27
  4.3 0.8 %copy-done = bf16[16,16,3,3,3]{1,0,4,3,2:T(8,128)(2,1)S(1)} copy-done((bf16[16,16,3,3,3]{1,0,4,3,2:T(8,128)(2,1)S(1)}, bf16[16,16,3,3,3]{1,0,4,3,2:T(8,128)(2,1)}, u32[]{:S(2)}) %copy-start) | copy-done | bytes 13848
  5.0 0.1 copy.26
  5.7 0.8 %copy-done.2 = bf16[16,16,3,3,3]{1,0,4,3,2:T(8,128)(2,1)S(1)} copy-done((bf16[16,16,3,3,3]{1,0,4,3,2:T(8,128)(2,1)S(1)}, bf16[16,16,3,3,3]{1,0,4,3,2:T(8,128)(2,1)}, u32[]{:S(2)}) %copy-start.2) | copy-done | bytes 13848
  6.7 0.7 %copy-done.4 = bf16[6,48,144]{2,1,0:T(8,128)(2,1)} copy-done((bf16[6,48,144]{2,1,0:T(8,128)(2,1)}, bf16[6,48,144]{2,1,0:T(8,128)(2,1)S(1)}, u32[]{:S(2)}) %copy-start.4) | copy-done | bytes 82968
  7.4 40.5 %shard_map.129 = (bf16[1,8,16,128]{3,2,1,0:T(8,128)(2,1)}, f32[8,16,128]{2,1,0:T(8,128)}, f32[192,128]{1,0:T(8,128)}, f32[192,128]{1,0:T(8,128)}) custom-call(s32[8,8]{1,0:T(8,128)} %bricks_ref.1, s32[8,8]{1,0:T(8,128)} %rows_ref.1, bf16[8,16,128]{2,1,0:T(8,128)(2,1)} %feats_ref.1, bf16[8,128,128]{2,1,0:T(8,128)(2,1)} %foot_ref.1, ...), custom_call_target="tpu_custom_call" | custom-call | tf_op jit(solution)/shard_map/pallas_call | solution.py:445
  47.9 0.7 %slice_bitcast_fusion = (f32[1,16,128]{2,1,0:T(8,128)S(1)}, f32[1,16,128]{2,1,0:T(8,128)S(1)}) fusion(f32[192,128]{1,0:T(8,128)} %get-tuple-element.11, f32[192,128]{1,0:T(8,128)} %get-tuple-element.10), kind=kLoop, calls=%fused_computation.12 | loop fusion | bytes 32768 | tf_op jit(solution)/shard_map/stack | solution.py:453
  48.6 0.9 %slice.15 = f32[144,48]{1,0:T(8,128)S(1)} slice(f32[192,128]{1,0:T(8,128)} %get-tuple-element.10), slice={[0:144], [0:48]} | slice | bytes 55296 | tf_op jit(solution)/shard_map/slice | solution.py:450
  49.7 0.6 %broadcast_multiply_fusion = f32[2,16]{1,0:T(2,128)} fusion(f32[2,16]{1,0:T(2,128)S(1)} %maximum_reduce_fusion), kind=kLoop, calls=%fused_computation.15 | loop fusion | flops 32 | bytes 256 | tf_op jit(solution)/shard_map/mul | solution.py:454
  50.2 0.2 copy-done.3
  50.6 0.2 stack.39
  50.8 0.2 stack.38
  51.0 0.2 stack.37
  51.2 0.3 fusion
  51.5 0.9 %copy.32 = f32[3,16,16,3,3,3]{2,1,5,4,3,0:T(8,128)} copy(f32[3,16,16,3,3,3]{2,4,3,1,5,0:T(4,128)S(1)} %fusion) | data formatting | bytes 165888
  52.4 0.6 %copy.40 = bf16[1,8,16,128]{3,2,1,0:T(8,128)(2,1)} copy(bf16[1,8,16,128]{3,2,1,0:T(8,128)(2,1)S(1)} %copy-done.6) | data formatting | bytes 65536
  53.0 0.2 copy-done.5
  53.3 0.6 %copy.41 = f32[8,16,128]{2,1,0:T(8,128)} copy(f32[8,16,128]{2,1,0:T(8,128)S(1)} %copy-done.5) | data formatting | bytes 131072
  (33 shorter events, 1.3 us)
Async XLA Ops:
  0.6 0.7 %copy-start.7 = (f32[16]{0:T(128)S(1)}, f32[16]{0:T(128)}, u32[]{:S(2)}) copy-start(f32[16]{0:T(128)} %param.18) | copy-start | bytes 196
  0.6 0.7 %copy-start.8 = (f32[16]{0:T(128)S(1)}, f32[16]{0:T(128)}, u32[]{:S(2)}) copy-start(f32[16]{0:T(128)} %param.17) | copy-start | bytes 196
  3.0 0.9 %copy-start.1 = (bf16[16,16,3,3,3]{1,0,4,3,2:T(8,128)(2,1)S(1)}, bf16[16,16,3,3,3]{1,0,4,3,2:T(8,128)(2,1)}, u32[]{:S(2)}) copy-start(bf16[16,16,3,3,3]{1,0,4,3,2:T(8,128)(2,1)} %param.15) | copy-start | bytes 41476
  4.1 0.9 %copy-start = (bf16[16,16,3,3,3]{1,0,4,3,2:T(8,128)(2,1)S(1)}, bf16[16,16,3,3,3]{1,0,4,3,2:T(8,128)(2,1)}, u32[]{:S(2)}) copy-start(bf16[16,16,3,3,3]{1,0,4,3,2:T(8,128)(2,1)} %param.16) | copy-start | bytes 41476
  5.6 0.9 %copy-start.2 = (bf16[16,16,3,3,3]{1,0,4,3,2:T(8,128)(2,1)S(1)}, bf16[16,16,3,3,3]{1,0,4,3,2:T(8,128)(2,1)}, u32[]{:S(2)}) copy-start(bf16[16,16,3,3,3]{1,0,4,3,2:T(8,128)(2,1)} %param.14) | copy-start | bytes 41476
  6.7 0.7 %copy-start.4 = (bf16[6,48,144]{2,1,0:T(8,128)(2,1)}, bf16[6,48,144]{2,1,0:T(8,128)(2,1)S(1)}, u32[]{:S(2)}) copy-start(bf16[6,48,144]{2,1,0:T(8,128)(2,1)S(1)} %constant_dynamic-update-slice_fusion.w_ref) | copy-start | bytes 248836
  49.5 0.9 %copy-start.3 = (f32[192,128]{1,0:T(8,128)S(1)}, f32[192,128]{1,0:T(8,128)}, u32[]{:S(2)}) copy-start(f32[192,128]{1,0:T(8,128)} %get-tuple-element.11) | copy-start | bytes 294916
  51.5 0.9 %copy-start.6 = (bf16[1,8,16,128]{3,2,1,0:T(8,128)(2,1)S(1)}, bf16[1,8,16,128]{3,2,1,0:T(8,128)(2,1)}, u32[]{:S(2)}) copy-start(bf16[1,8,16,128]{3,2,1,0:T(8,128)(2,1)} %get-tuple-element.24) | copy-start | bytes 98308
  52.4 0.9 %copy-start.5 = (f32[8,16,128]{2,1,0:T(8,128)S(1)}, f32[8,16,128]{2,1,0:T(8,128)}, u32[]{:S(2)}) copy-start(f32[8,16,128]{2,1,0:T(8,128)} %get-tuple-element.25) | copy-start | bytes 196612
where the time goes:
time: 54.3 us; the launch traced here: 53.9 us
  Pallas kernels  40.5 us (75%)
  local copies, waits for them, and re-layouts  11.6 us (21%)
  other arithmetic  0.99 us (2%)
  between operations  0.85 us (2%)
    pallas_call x1, Pallas kernels, body(): call(tile_bricks, tile_rows, camera_feats, footprint_slot_weights, weight...  40.5 us
    unnamed x26, local copies, waits for them, and re-layouts  6.15 us
    transpose x6, local copies, waits for them, and re-layouts, backward_matrix(): jnp.transpose(jnp.flip(weight, (2, 3, 4)), (4, 1, 2, 3, 0))  1.35 us

commit v1 on v0

--- a/solution.py
+++ b/solution.py
@@ -12,7 +12,7 @@
 BF16 = jnp.bfloat16
 DIRS = [(dz, dy) for dz in (-1, 0, 1) for dy in (0, -1, 1) if (dz, dy) != (0, 0)]
 LIFT, ACT1, ACT2, OUTG, BACK2, BACK1 = range(6)
-BIAS_ROWS = 16
+PARAMS = {"vmem_limit_bytes": 16 * 1024 * 1024}
 
 
 def round_up(value, step):
@@ -29,13 +29,15 @@
     wrows = 9 * channels
     srows = 3 * channels
     cells = rows_y * channels
-    total_rows = wrows + BIAS_ROWS
-    piece = round_up(-(-total_rows // depths), 8)
+    half = 2 * srows
+    sizes = (2 * half, half)
+    pieces = tuple(round_up(-(-size // depths), 8) for size in sizes)
+    piece_max = max(pieces)
 
     def kernel(
-        bricks_ref, rows_ref, feats_ref, foot_ref, w_ref, bias_ref, outg_ref,
+        bricks_ref, rows_ref, feats_ref, foot_ref, w1_ref, w2_ref, w3_ref, bias1_ref, bias2_ref, outg_ref,
         field_ref, camera_ref, early_out, late_out,
-        vol, part, rsbuf, grid, own_sum, ar_rs, ar_mid,
+        w_ref, vol, part, rsbuf, grid, own_sum, ar_rs, ar_mid,
         halo_send, halo_recv, view_send, view_recv, ar_send, ar_recv,
     ):
         d = lax.axis_index("depth")
@@ -164,6 +166,13 @@
             part_copy(k).start()
         halo_start(OUTG)
 
+        for n, ref in enumerate((w1_ref, w2_ref, w3_ref)):
+            tiles_f = [ref[t].astype(F32) for t in range(27)]
+            ahead = [jnp.concatenate([tiles_f[3 * ab + c] for c in range(3)], axis=0) for ab in range(9)]
+            w_ref[n] = jnp.concatenate(ahead, axis=1).astype(BF16)
+            back = [jnp.concatenate([tiles_f[26 - 3 * ab - c] for ab in range(9)], axis=0) for c in range(3)]
+            w_ref[5 - n] = jnp.concatenate([tile.T for tile in back], axis=0).astype(BF16)
+
         def im2col(index):
             columns = []
             for y in range(rows_y):
@@ -201,19 +210,20 @@
 
         def weight_grad(columns, pieces):
             stacked = jnp.concatenate(pieces, axis=0)
-            return lax.dot_general(columns, stacked, (((1,), (1,)), ((), ())), preferred_element_type=F32)
-
-        def blank(rows):
-            return jnp.zeros((rows, rows_y * width), BF16)
+            return lax.dot_general(stacked, columns, (((1,), (1,)), ((), ())), preferred_element_type=F32)
 
         def rows_sum(values):
             total = values[0:channels]
             for y in range(1, rows_y):
                 total = total + values[y * channels:(y + 1) * channels]
-            return total
-
-        def tall_bias(n):
-            return jnp.concatenate([bias_ref[n]] * rows_y, axis=0)
+            return jnp.sum(total, axis=1, keepdims=True)
+
+        def tall_bias(ref):
+            shape = (cells, channels)
+            diagonal = lax.rem(lax.broadcasted_iota(jnp.int32, shape, 0), channels)
+            diagonal = diagonal == lax.broadcasted_iota(jnp.int32, shape, 1)
+            spread = jnp.broadcast_to(ref[...], shape)
+            return jnp.sum(jnp.where(diagonal, spread, 0.0), axis=1, keepdims=True)
 
         def put(index, values):
             vol[index, 1, pl.ds(1, rows_y)] = values.reshape(rows_y, channels, width)
@@ -223,7 +233,7 @@
         def ar_a(n, k):
             to = lax.rem(d + k, depths)
             return pltpu.make_async_remote_copy(
-                src_ref=own_sum.at[n, pl.ds(pl.multiple_of(to * piece, 8), piece)], dst_ref=ar_rs.at[n, k],
+                src_ref=own_sum.at[n, pl.ds(pl.multiple_of(to * pieces[n], 8), pieces[n])], dst_ref=ar_rs.at[n, k, pl.ds(0, pieces[n])],
                 send_sem=ar_send.at[n, 0, k], recv_sem=ar_recv.at[n, 0, k],
                 device_id={"depth": to}, device_id_type=MESH,
             )
@@ -231,7 +241,7 @@
         def ar_b(n, k):
             to, peer = group_peers[k - 1]
             return pltpu.make_async_remote_copy(
-                src_ref=ar_mid.at[n, me], dst_ref=ar_mid.at[n, me],
+                src_ref=ar_mid.at[n, me, pl.ds(0, pieces[n])], dst_ref=ar_mid.at[n, me, pl.ds(0, pieces[n])],
                 send_sem=ar_send.at[n, 1, k], recv_sem=ar_recv.at[n, 1, k],
                 device_id=peer, device_id_type=MESH,
             )
@@ -239,45 +249,53 @@
         def ar_b_in(n, k):
             source = lax.rem(me + group - k, group)
             return pltpu.make_async_remote_copy(
-                src_ref=ar_mid.at[n, source], dst_ref=ar_mid.at[n, source],
+                src_ref=ar_mid.at[n, source, pl.ds(0, pieces[n])], dst_ref=ar_mid.at[n, source, pl.ds(0, pieces[n])],
                 send_sem=ar_send.at[n, 1, k], recv_sem=ar_recv.at[n, 1, k],
                 device_id=group_peers[k - 1][1], device_id_type=MESH,
             )
 
         def ar_c(n, k, owner):
             to = lax.rem(d + k, depths)
-            place = outs[n].at[pl.ds(pl.multiple_of(owner * piece, 8), piece)]
+            place = outs[n].at[pl.ds(pl.multiple_of(owner * pieces[n], 8), pieces[n])]
             return pltpu.make_async_remote_copy(
                 src_ref=place, dst_ref=place,
                 send_sem=ar_send.at[n, 2, k], recv_sem=ar_recv.at[n, 2, k],
                 device_id={"depth": to}, device_id_type=MESH,
             )
 
-        def reduce_start(n, values, bias):
-            own_sum[n, pl.ds(0, wrows)] = values
-            own_sum[n, pl.ds(wrows, BIAS_ROWS)] = bias
-            if depths * piece > total_rows:
-                rest = depths * piece - total_rows
-                own_sum[n, pl.ds(total_rows, rest)] = jnp.zeros((rest, 128), F32)
+        def keep_grad(n, base, values, bias=None):
+            main = 128
+            own_sum[n, pl.ds(base, srows)] = values[:, :main]
+            own_sum[n, pl.ds(base + srows, srows)] = jnp.zeros((srows, 128), F32)
+            own_sum[n, pl.ds(base + srows, srows), pl.ds(0, wrows - main)] = values[:, main:]
+            if bias is not None:
+                place = pl.ds(base + srows, channels)
+                lanes = lax.broadcasted_iota(jnp.int32, (channels, 128), 1)
+                own_sum[n, place] = jnp.where(lanes == wrows - main, bias, own_sum[n, place])
+
+        def reduce_start(n):
+            rest = depths * pieces[n] - sizes[n]
+            if rest:
+                own_sum[n, pl.ds(sizes[n], rest)] = jnp.zeros((rest, 128), F32)
             for k in range(1, depths):
                 ar_a(n, k).start()
 
         def reduce_middle(n):
-            total = own_sum[n, pl.ds(pl.multiple_of(d * piece, 8), piece)]
+            total = own_sum[n, pl.ds(pl.multiple_of(d * pieces[n], 8), pieces[n])]
             for k in range(1, depths):
                 ar_a(n, k).wait_recv()
-                total = total + ar_rs[n, k]
-            ar_mid[n, me] = total
+                total = total + ar_rs[n, k, pl.ds(0, pieces[n])]
+            ar_mid[n, me, pl.ds(0, pieces[n])] = total
             for k in range(1, group):
                 ar_b(n, k).start()
 
         def reduce_last(n):
             for k in range(1, group):
                 ar_b_in(n, k).wait_recv()
-            total = ar_mid[n, 0]
+            total = ar_mid[n, 0, pl.ds(0, pieces[n])]
             for j in range(1, group):
-                total = total + ar_mid[n, j]
-            outs[n][pl.ds(pl.multiple_of(d * piece, 8), piece)] = total
+                total = total + ar_mid[n, j, pl.ds(0, pieces[n])]
+            outs[n][pl.ds(pl.multiple_of(d * pieces[n], 8), pieces[n])] = total
             for k in range(1, depths):
                 ar_c(n, k, d).start()
 
@@ -304,7 +322,7 @@
         out_pieces = grad_rows(outg_ref[0].reshape(cells, width))
 
         halo_wait(LIFT)
-        pre_first = conv(0, im2col(LIFT)) + tall_bias(0)
+        pre_first = conv(0, im2col(LIFT)) + tall_bias(bias1_ref)
         act_first = jax.nn.silu(pre_first).astype(BF16)
         put(ACT1, act_first)
         halo_start(ACT1)
@@ -312,7 +330,7 @@
 
         halo_wait(ACT1)
         columns_second = im2col(ACT1)
-        pre_second = conv(1, columns_second) + tall_bias(1)
+        pre_second = conv(1, columns_second) + tall_bias(bias2_ref)
         slope_second = up_second * silu_grad(pre_second)
         back_second = slope_second.astype(BF16)
         put(BACK2, back_second)
@@ -320,7 +338,8 @@
         act_second = (jax.nn.silu(pre_second) + act_first.astype(F32)).astype(BF16)
         put(ACT2, act_second)
         halo_start(ACT2)
-        early = weight_grad(columns_second, grad_rows(back_second) + [blank(128 - srows)])
+        early = weight_grad(columns_second, grad_rows(back_second))
+        keep_grad(0, 0, early, rows_sum(slope_second))
 
         halo_wait(BACK2)
         up_first = up_second + conv(4, im2col(BACK2))
@@ -328,17 +347,16 @@
         back_first = slope_first.astype(BF16)
         put(BACK1, back_first)
         halo_start(BACK1)
-        late = weight_grad(im2col(LIFT), grad_rows(back_first) + [blank(128 - srows)])
-        reduce_start(1, late, rows_sum(slope_first))
+        late = weight_grad(im2col(LIFT), grad_rows(back_first))
+        keep_grad(1, 0, late, rows_sum(slope_first))
+        reduce_start(1)
 
         halo_wait(ACT2)
         columns_third = im2col(ACT2)
         field = conv(2, columns_third)
         field_ref[0] = field.astype(BF16).reshape(rows_y, channels, width)
-        early = early + weight_grad(
-            columns_third, [blank(srows)] + out_pieces + [blank(128 - 2 * srows)]
-        )
-        reduce_start(0, early, rows_sum(slope_second))
+        keep_grad(0, half, weight_grad(columns_third, out_pieces))
+        reduce_start(0)
 
         halo_wait(BACK1)
         lift_grad = conv(5, im2col(BACK1)).astype(BF16)
@@ -384,19 +402,20 @@
         out_shape=(
             jax.ShapeDtypeStruct((1,) + plane, BF16),
             jax.ShapeDtypeStruct((tiles, channels, width), F32),
-            jax.ShapeDtypeStruct((depths * piece, 128), F32),
-            jax.ShapeDtypeStruct((depths * piece, 128), F32),
+            jax.ShapeDtypeStruct((depths * pieces[0], 128), F32),
+            jax.ShapeDtypeStruct((depths * pieces[1], 128), F32),
         ),
-        in_specs=[smem, smem] + [vmem] * 5,
+        in_specs=[smem, smem] + [vmem] * 8,
         out_specs=(vmem,) * 4,
         scratch_shapes=[
+            pltpu.VMEM((6, srows, wrows), BF16),
             pltpu.VMEM((6, 3, rows_y + 2, channels, width), BF16),
             pltpu.VMEM((views,) + plane, BF16),
             pltpu.VMEM((views,) + plane, BF16),
             pltpu.VMEM((views,) + plane, BF16),
-            pltpu.VMEM((2, depths * piece, 128), F32),
-            pltpu.VMEM((2, depths, piece, 128), F32),
-            pltpu.VMEM((2, group, piece, 128), F32),
+            pltpu.VMEM((2, depths * piece_max, 128), F32),
+            pltpu.VMEM((2, depths, piece_max, 128), F32),
+            pltpu.VMEM((2, group, piece_max, 128), F32),
             pltpu.SemaphoreType.DMA((6, len(DIRS))),
             pltpu.SemaphoreType.DMA((6, len(DIRS))),
             pltpu.SemaphoreType.DMA((2, views)),
@@ -404,18 +423,49 @@
             pltpu.SemaphoreType.DMA((2, 3, max(depths, group))),
             pltpu.SemaphoreType.DMA((2, 3, max(depths, group))),
         ],
-        compiler_params=pltpu.CompilerParams(collective_id=0, has_side_effects=True),
+        compiler_params=pltpu.CompilerParams(collective_id=0, has_side_effects=True, **PARAMS),
     )
 
 
-def forward_matrix(weight):
+def finish(field, camera, early, late, scale, channels):
+    wrows, srows = 9 * channels, 3 * channels
+
+    def kernel(field_in, camera_in, early_ref, late_ref, field_ref, camera_ref, grads_ref, bias_ref):
+        field_ref[...] = field_in[...]
+        camera_ref[...] = camera_in[...]
+        per_row = 128 // channels
+        for n, (ref, base) in enumerate(((late_ref, 0), (early_ref, 0), (early_ref, 2 * srows))):
+            for ab in range(9):
+                rows = base + srows * (ab // per_row)
+                lanes = channels * (ab % per_row)
+                tile = ref[pl.ds(rows, srows), pl.ds(lanes, channels)] * scale
+                for c in range(3):
+                    grads_ref[n, 3 * ab + c] = tile[c * channels:(c + 1) * channels]
+            if n < 2:
+                column = ref[pl.ds(base + srows, channels), pl.ds(wrows - 128, 1)] * scale
+                shape = (channels, channels)
+                diagonal = lax.broadcasted_iota(jnp.int32, shape, 0) == lax.broadcasted_iota(jnp.int32, shape, 1)
+                spread = jnp.where(diagonal, jnp.broadcast_to(column, shape), 0.0)
+                bias_ref[pl.ds(n, 1)] = jnp.sum(spread, axis=0, keepdims=True)
+
+    vmem = pl.BlockSpec(memory_space=pltpu.VMEM)
+    return pl.pallas_call(
+        kernel,
+        out_shape=(
+            jax.ShapeDtypeStruct(field.shape, field.dtype),
+            jax.ShapeDtypeStruct(camera.shape, camera.dtype),
+            jax.ShapeDtypeStruct((3, 27, channels, channels), F32),
+            jax.ShapeDtypeStruct((2, channels), F32),
+        ),
+        in_specs=[vmem] * 4,
+        out_specs=(vmem,) * 4,
+        compiler_params=pltpu.CompilerParams(**PARAMS),
+    )(field, camera, early, late)
+
+
+def tap_tiles(weight):
     c = weight.shape[0]
-    return jnp.transpose(weight, (4, 0, 2, 3, 1)).reshape(3 * c, 9 * c)
-
-
-def backward_matrix(weight):
-    c = weight.shape[0]
-    return jnp.transpose(jnp.flip(weight, (2, 3, 4)), (4, 1, 2, 3, 0)).reshape(3 * c, 9 * c)
+    return jnp.transpose(weight, (2, 3, 4, 0, 1)).reshape(27, c, c)
 
 
 def body(
@@ -434,24 +484,16 @@
     tiles, channels, _ = camera_feats.shape
     slots, width, _ = footprint_slot_weights.shape
     rows_y = out_grad.shape[1]
-    weights = jnp.stack(
-        [forward_matrix(w) for w in (conv_first, conv_second, conv_third)]
-        + [backward_matrix(w) for w in (conv_third, conv_second, conv_first)]
-    )
-    biases = jnp.broadcast_to(
-        jnp.stack([bias_first, bias_second])[:, :, None], (2, channels, width)
-    )
     call = make_kernel(depths, heights, views, tiles, slots, rows_y, channels, width)
     field, camera, early, late = call(
-        tile_bricks, tile_rows, camera_feats, footprint_slot_weights, weights, biases, out_grad
+        tile_bricks, tile_rows, camera_feats, footprint_slot_weights,
+        tap_tiles(conv_first), tap_tiles(conv_second), tap_tiles(conv_third),
+        bias_first[None], bias_second[None], out_grad,
     )
     scale = 1.0 / math.sqrt(rows_y * width * depths * heights * views)
-    wrows, srows = 9 * channels, 3 * channels
-    parts = jnp.stack([late[:wrows, :srows], early[:wrows, :srows], early[:wrows, srows:2 * srows]])
-    parts = parts.reshape(3, 3, 3, channels, 3, channels) * scale
-    weight_grads = jnp.transpose(parts, (0, 5, 3, 1, 2, 4))
-    sums = jnp.stack([late[wrows:wrows + channels], early[wrows:wrows + channels]])
-    return field, camera, weight_grads, jnp.sum(sums, axis=2) * scale
+    field, camera, grads, biases = finish(field, camera, early, late, scale, channels)
+    grads = grads.reshape(3, 3, 3, 3, channels, channels)
+    return field, camera, jnp.transpose(grads, (0, 4, 5, 1, 2, 3)), biases
 
 
 def solution(mesh):

time: 54.3 us -> 46.4 us (0.85)
  local copies, waits for them, and re-layouts: 11.6 us -> 5.83 us
  Pallas kernels: 40.5 us -> 39.5 us
  other arithmetic: 0.99 us -> 0 us
    another operation x11 -> x0, local copies, waits for them, and re-layouts: 2.03 us -> none  [the longest x7 0.8 us: body(): jnp.stack([forward_matrix(w) for w in (conv_first, conv_second, conv_thir...]
    transpose x9 -> x0, local copies, waits for them, and re-layouts: 1.53 us -> none  [the longest x6 1.35 us: backward_matrix(): jnp.transpose(jnp.flip(weight, (2, 3, 4)), (4, 1, 2, 3, 0))]
    slice x5 -> x0, local copies, waits for them, and re-layouts: 1.18 us -> none  [the longest x2 0.96 us: body(): late[:wrows, :srows]]
    pallas_call x1 -> x2, Pallas kernels: 40.5 us -> 39.5 us  [the longest x1 38.5 us: body(): call(tile_bricks, tile_rows, camera_feats, footprint_slot_weights, tap_ti...]
    broadcast_in_dim x1 -> x0, local copies, waits for them, and re-layouts: 0.68 us -> none  [body(): jnp.broadcast_to(jnp.stack([bias_first, bias_second])[:, :, None], (2, ch...]
    mul x1 -> x0, other arithmetic: 0.58 us -> none  [body(): return (field, camera, weight_grads, jnp.sum(sums, axis=2) * scale)]
    unnamed x26 -> x20, local copies, waits for them, and re-layouts: 6.15 us -> 5.83 us
where the time goes in v1:
time: 46.4 us; the launch traced here: 46 us
  Pallas kernels  39.5 us (85%)
  local copies, waits for them, and re-layouts  5.83 us (13%)
  between operations  0.68 us (1%)
    pallas_call x1, Pallas kernels, body(): call(tile_bricks, tile_rows, camera_feats, footprint_slot_weights, tap_ti...  38.5 us
    unnamed x20, local copies, waits for them, and re-layouts  5.83 us
    pallas_call x1, Pallas kernels, finish(): pl.pallas_call(kernel, out_shape=(jax.ShapeDtypeStruct(field.shape, field...  1.05 us

profile of v1, /device:TPU:0, one launch (start us, length us, event | category | flops | bytes accessed | tf_op | source)
XLA Modules:
  0.0 46.0 jit_solution(17728875395101960610)
XLA Ops:
  0.6 0.0 copy-start.7
  0.6 0.0 copy-start.6
  0.7 0.0 copy-start.8
  0.7 0.0 copy-start.9
  0.7 0.6 %copy-done.7 = s32[8,8]{1,0:T(8,128)S(1)} copy-done((s32[8,8]{1,0:T(8,128)S(1)}, s32[8,8]{1,0:T(8,128)}, u32[]{:S(2)}) %copy-start.7) | copy-done | bytes 280
  1.3 0.0 copy-done.6
  1.3 0.0 copy-done.8
  1.3 0.0 copy-done.9
  1.3 0.0 copy-start
  1.3 0.9 %copy-done = bf16[8,128,128]{2,1,0:T(8,128)(2,1)S(1)} copy-done((bf16[8,128,128]{2,1,0:T(8,128)(2,1)S(1)}, bf16[8,128,128]{2,1,0:T(8,128)(2,1)}, u32[]{:S(2)}) %copy-start) | copy-done | bytes 262168
  2.3 0.0 copy-start.1
  2.3 0.9 %copy-done.1 = bf16[16,16,3,3,3]{1,0,4,3,2:T(8,128)(2,1)S(1)} copy-done((bf16[16,16,3,3,3]{1,0,4,3,2:T(8,128)(2,1)S(1)}, bf16[16,16,3,3,3]{1,0,4,3,2:T(8,128)(2,1)}, u32[]{:S(2)}) %copy-start.1) | copy-done | bytes 13848
  3.2 0.0 copy-start.2
  3.2 0.9 %copy-done.2 = bf16[16,16,3,3,3]{1,0,4,3,2:T(8,128)(2,1)S(1)} copy-done((bf16[16,16,3,3,3]{1,0,4,3,2:T(8,128)(2,1)S(1)}, bf16[16,16,3,3,3]{1,0,4,3,2:T(8,128)(2,1)}, u32[]{:S(2)}) %copy-start.2) | copy-done | bytes 13848
  4.1 0.0 copy-start.3
  4.1 0.9 %copy-done.3 = bf16[16,16,3,3,3]{1,0,4,3,2:T(8,128)(2,1)S(1)} copy-done((bf16[16,16,3,3,3]{1,0,4,3,2:T(8,128)(2,1)S(1)}, bf16[16,16,3,3,3]{1,0,4,3,2:T(8,128)(2,1)}, u32[]{:S(2)}) %copy-start.3) | copy-done | bytes 13848
  5.0 0.0 copy-start.4
  5.0 0.8 %copy-done.4 = bf16[8,16,128]{2,1,0:T(8,128)(2,1)S(1)} copy-done((bf16[8,16,128]{2,1,0:T(8,128)(2,1)S(1)}, bf16[8,16,128]{2,1,0:T(8,128)(2,1)}, u32[]{:S(2)}) %copy-start.4) | copy-done | bytes 32792
  5.7 0.0 copy-start.5
  5.7 0.8 %copy-done.5 = bf16[1,8,16,128]{3,2,1,0:T(8,128)(2,1)S(1)} copy-done((bf16[1,8,16,128]{3,2,1,0:T(8,128)(2,1)S(1)}, bf16[1,8,16,128]{3,2,1,0:T(8,128)(2,1)}, u32[]{:S(2)}) %copy-start.5) | copy-done | bytes 32792
  6.5 38.5 %shard_map.129 = (bf16[1,8,16,128]{3,2,1,0:T(8,128)(2,1)S(1)}, f32[8,16,128]{2,1,0:T(8,128)S(1)}, f32[192,128]{1,0:T(8,128)S(1)}, f32[128,128]{1,0:T(8,128)S(1)}) custom-call(s32[8,8]{1,0:T(8,128)S(1)} %copy-done.6, s32[8,8]{1,0:T(8,128)S(1)} %copy-done.7, bf16[8,16,128]{2,1,0:T(8,128)(2,1)S(1)} %copy-done.4, bf16[8,128,128]{2,1,0:T(8,128)(2,1)S(1)} %copy-done, ...), custom_call_target="tpu_custom_call" | custom-call | tf_op jit(solution)/shard_map/pallas_call | solution.py:488
  45.0 1.0 %shard_map.130 = (bf16[1,8,16,128]{3,2,1,0:T(8,128)(2,1)}, f32[8,16,128]{2,1,0:T(8,128)}, f32[3,27,16,16]{3,2,1,0:T(8,128)}, f32[2,16]{1,0:T(2,128)}) custom-call(bf16[1,8,16,128]{3,2,1,0:T(8,128)(2,1)S(1)} %get-tuple-element.12.field_in, f32[8,16,128]{2,1,0:T(8,128)S(1)} %get-tuple-element.13.camera_in, f32[192,128]{1,0:T(8,128)S(1)} %get-tuple-element.14.early_ref, ...), custom_call_target="tpu_custom_call" | custom-call | tf_op jit(solution)/shard_map/pallas_call | solution.py:452
Async XLA Ops:
  0.6 0.7 %copy-start.7 = (s32[8,8]{1,0:T(8,128)S(1)}, s32[8,8]{1,0:T(8,128)}, u32[]{:S(2)}) copy-start(s32[8,8]{1,0:T(8,128)} %rows_ref.1) | copy-start | bytes 772
  0.6 0.7 %copy-start.6 = (s32[8,8]{1,0:T(8,128)S(1)}, s32[8,8]{1,0:T(8,128)}, u32[]{:S(2)}) copy-start(s32[8,8]{1,0:T(8,128)} %bricks_ref.1) | copy-start | bytes 772
  0.7 0.7 %copy-start.8 = (f32[16]{0:T(128)S(1)}, f32[16]{0:T(128)}, u32[]{:S(2)}) copy-start(f32[16]{0:T(128)} %param.17) | copy-start | bytes 196
  0.7 0.7 %copy-start.9 = (f32[16]{0:T(128)S(1)}, f32[16]{0:T(128)}, u32[]{:S(2)}) copy-start(f32[16]{0:T(128)} %param.18) | copy-start | bytes 196
  1.3 1.0 %copy-start = (bf16[8,128,128]{2,1,0:T(8,128)(2,1)S(1)}, bf16[8,128,128]{2,1,0:T(8,128)(2,1)}, u32[]{:S(2)}) copy-start(bf16[8,128,128]{2,1,0:T(8,128)(2,1)} %foot_ref.1) | copy-start | bytes 786436
  2.3 0.9 %copy-start.1 = (bf16[16,16,3,3,3]{1,0,4,3,2:T(8,128)(2,1)S(1)}, bf16[16,16,3,3,3]{1,0,4,3,2:T(8,128)(2,1)}, u32[]{:S(2)}) copy-start(bf16[16,16,3,3,3]{1,0,4,3,2:T(8,128)(2,1)} %param.14) | copy-start | bytes 41476
  3.2 0.9 %copy-start.2 = (bf16[16,16,3,3,3]{1,0,4,3,2:T(8,128)(2,1)S(1)}, bf16[16,16,3,3,3]{1,0,4,3,2:T(8,128)(2,1)}, u32[]{:S(2)}) copy-start(bf16[16,16,3,3,3]{1,0,4,3,2:T(8,128)(2,1)} %param.15) | copy-start | bytes 41476
  4.1 0.9 %copy-start.3 = (bf16[16,16,3,3,3]{1,0,4,3,2:T(8,128)(2,1)S(1)}, bf16[16,16,3,3,3]{1,0,4,3,2:T(8,128)(2,1)}, u32[]{:S(2)}) copy-start(bf16[16,16,3,3,3]{1,0,4,3,2:T(8,128)(2,1)} %param.16) | copy-start | bytes 41476
  5.0 0.8 %copy-start.4 = (bf16[8,16,128]{2,1,0:T(8,128)(2,1)S(1)}, bf16[8,16,128]{2,1,0:T(8,128)(2,1)}, u32[]{:S(2)}) copy-start(bf16[8,16,128]{2,1,0:T(8,128)(2,1)} %feats_ref.1) | copy-start | bytes 98308
  5.7 0.8 %copy-start.5 = (bf16[1,8,16,128]{3,2,1,0:T(8,128)(2,1)S(1)}, bf16[1,8,16,128]{3,2,1,0:T(8,128)(2,1)}, u32[]{:S(2)}) copy-start(bf16[1,8,16,128]{3,2,1,0:T(8,128)(2,1)} %outg_ref.1) | copy-start | bytes 98308

commit v2 on v1

--- a/solution.py
+++ b/solution.py
@@ -12,7 +12,7 @@
 BF16 = jnp.bfloat16
 DIRS = [(dz, dy) for dz in (-1, 0, 1) for dy in (0, -1, 1) if (dz, dy) != (0, 0)]
 LIFT, ACT1, ACT2, OUTG, BACK2, BACK1 = range(6)
-PARAMS = {"vmem_limit_bytes": 16 * 1024 * 1024}
+PARAMS = {"vmem_limit_bytes": 65150 * 1024}
 
 
 def round_up(value, step):
@@ -35,11 +35,26 @@
     piece_max = max(pieces)
 
     def kernel(
-        bricks_ref, rows_ref, feats_ref, foot_ref, w1_ref, w2_ref, w3_ref, bias1_ref, bias2_ref, outg_ref,
+        bricks_hbm, rows_hbm, feats_hbm, foot_hbm, w1_hbm, w2_hbm, w3_hbm, bias1_hbm, bias2_hbm, outg_hbm,
         field_ref, camera_ref, early_out, late_out,
+        bricks_ref, rows_ref, feats_ref, foot_ref, w1_ref, w2_ref, w3_ref, bias1_ref, bias2_ref, in_sem,
         w_ref, vol, part, rsbuf, grid, own_sum, ar_rs, ar_mid,
         halo_send, halo_recv, view_send, view_recv, ar_send, ar_recv,
     ):
+        sources = (
+            bricks_hbm, rows_hbm, feats_hbm, foot_hbm, outg_hbm.at[0],
+            w1_hbm, w2_hbm, w3_hbm, bias1_hbm, bias2_hbm,
+        )
+        places = (
+            bricks_ref, rows_ref, feats_ref, foot_ref, vol.at[OUTG, 1, pl.ds(1, rows_y)],
+            w1_ref, w2_ref, w3_ref, bias1_ref, bias2_ref,
+        )
+        loads = [
+            pltpu.make_async_copy(source, place, in_sem.at[n])
+            for n, (source, place) in enumerate(zip(sources, places))
+        ]
+        for load in loads:
+            load.start()
         d = lax.axis_index("depth")
         h = lax.axis_index("height")
         v = lax.axis_index("view")
@@ -127,7 +142,8 @@
                 for index in range(6):
                     slot = halo_slot(index, dz, dy)
                     slot[...] = jnp.zeros(slot.shape, BF16)
-        vol[OUTG, 1, pl.ds(1, rows_y)] = outg_ref[0]
+        for load in loads[:4]:
+            load.wait()
 
         nrow = views * rows_y
         lane = lax.broadcasted_iota(jnp.int32, (1, tiles * channels), 1)
@@ -164,7 +180,10 @@
 
         for k in range(1, views):
             part_copy(k).start()
+        loads[4].wait()
         halo_start(OUTG)
+        for load in loads[5:]:
+            load.wait()
 
         for n, ref in enumerate((w1_ref, w2_ref, w3_ref)):
             tiles_f = [ref[t].astype(F32) for t in range(27)]
@@ -319,7 +338,7 @@
 
         halo_wait(OUTG)
         up_second = conv(3, im2col(OUTG))
-        out_pieces = grad_rows(outg_ref[0].reshape(cells, width))
+        out_pieces = grad_rows(vol[OUTG, 1, pl.ds(1, rows_y)].reshape(cells, width))
 
         halo_wait(LIFT)
         pre_first = conv(0, im2col(LIFT)) + tall_bias(bias1_ref)
@@ -395,7 +414,7 @@
             reduce_drain(n)
 
     vmem = pl.BlockSpec(memory_space=pltpu.VMEM)
-    smem = pl.BlockSpec(memory_space=pltpu.SMEM)
+    hbm = pl.BlockSpec(memory_space=pltpu.HBM)
     plane = (rows_y, channels, width)
     return pl.pallas_call(
         kernel,
@@ -405,9 +424,19 @@
             jax.ShapeDtypeStruct((depths * pieces[0], 128), F32),
             jax.ShapeDtypeStruct((depths * pieces[1], 128), F32),
         ),
-        in_specs=[smem, smem] + [vmem] * 8,
+        in_specs=[hbm] * 10,
         out_specs=(vmem,) * 4,
         scratch_shapes=[
+            pltpu.SMEM((tiles, slots), jnp.int32),
+            pltpu.SMEM((tiles, slots), jnp.int32),
+            pltpu.VMEM((tiles, channels, width), BF16),
+            pltpu.VMEM((slots, width, width), BF16),
+            pltpu.VMEM((27, channels, channels), BF16),
+            pltpu.VMEM((27, channels, channels), BF16),
+            pltpu.VMEM((27, channels, channels), BF16),
+            pltpu.VMEM((1, channels), F32),
+            pltpu.VMEM((1, channels), F32),
+            pltpu.SemaphoreType.DMA((10,)),
             pltpu.VMEM((6, srows, wrows), BF16),
             pltpu.VMEM((6, 3, rows_y + 2, channels, width), BF16),
             pltpu.VMEM((views,) + plane, BF16),

time: 46.4 us -> 41.4 us (0.89)
  local copies, waits for them, and re-layouts: 5.83 us -> 0 us
  Pallas kernels: 39.5 us -> 40.6 us
    unnamed x20 -> x0, local copies, waits for them, and re-layouts: 5.83 us -> none
    pallas_call x1, Pallas kernels: 1.05 us -> 2 us  [finish(): pl.pallas_call(kernel, out_shape=(jax.ShapeDtypeStruct(field.shape, field...]
where the time goes in v2:
time: 41.4 us; the launch traced here: 41.2 us
  Pallas kernels  40.6 us (98%)
  between operations  0.64 us (2%)
    pallas_call x1, Pallas kernels, body(): call(tile_bricks, tile_rows, camera_feats, footprint_slot_weights, tap_ti...  38.6 us
    pallas_call x1, Pallas kernels, finish(): pl.pallas_call(kernel, out_shape=(jax.ShapeDtypeStruct(field.shape, field...  2 us

profile of v2, /device:TPU:0, one launch (start us, length us, event | category | flops | bytes accessed | tf_op | source)
XLA Modules:
  0.0 41.2 jit_solution(4494472832416052270)
XLA Ops:
  0.6 38.6 %shard_map.129 = (bf16[1,8,16,128]{3,2,1,0:T(8,128)(2,1)}, f32[8,16,128]{2,1,0:T(8,128)}, f32[192,128]{1,0:T(8,128)}, f32[128,128]{1,0:T(8,128)}) custom-call(s32[8,8]{1,0:T(8,128)} %bricks_hbm.1, s32[8,8]{1,0:T(8,128)} %rows_hbm.1, bf16[8,16,128]{2,1,0:T(8,128)(2,1)} %feats_hbm.1, bf16[8,128,128]{2,1,0:T(8,128)(2,1)} %foot_hbm.1, ...), custom_call_target="tpu_custom_call" | custom-call | tf_op jit(solution)/shard_map/pallas_call | solution.py:517
  39.2 2.0 %shard_map.130 = (bf16[1,8,16,128]{3,2,1,0:T(8,128)(2,1)}, f32[8,16,128]{2,1,0:T(8,128)}, f32[3,27,16,16]{3,2,1,0:T(8,128)}, f32[2,16]{1,0:T(2,128)}) custom-call(bf16[1,8,16,128]{3,2,1,0:T(8,128)(2,1)} %get-tuple-element.12.field_in, f32[8,16,128]{2,1,0:T(8,128)} %get-tuple-element.13.camera_in, f32[192,128]{1,0:T(8,128)} %get-tuple-element.14.early_ref, ...), custom_call_target="tpu_custom_call" | custom-call | tf_op jit(solution)/shard_map/pallas_call | solution.py:481

commit v3 on v2

--- a/solution.py
+++ b/solution.py
@@ -38,7 +38,7 @@
         bricks_hbm, rows_hbm, feats_hbm, foot_hbm, w1_hbm, w2_hbm, w3_hbm, bias1_hbm, bias2_hbm, outg_hbm,
         field_ref, camera_ref, early_out, late_out,
         bricks_ref, rows_ref, feats_ref, foot_ref, w1_ref, w2_ref, w3_ref, bias1_ref, bias2_ref, in_sem,
-        w_ref, vol, part, rsbuf, grid, own_sum, ar_rs, ar_mid,
+        outg_ref, field_own, field_in, swap_send, swap_recv, w_ref, vol, part, rsbuf, grid, own_sum, ar_rs, ar_mid,
         halo_send, halo_recv, view_send, view_recv, ar_send, ar_recv,
     ):
         sources = (
@@ -46,7 +46,7 @@
             w1_hbm, w2_hbm, w3_hbm, bias1_hbm, bias2_hbm,
         )
         places = (
-            bricks_ref, rows_ref, feats_ref, foot_ref, vol.at[OUTG, 1, pl.ds(1, rows_y)],
+            bricks_ref, rows_ref, feats_ref, foot_ref, outg_ref,
             w1_ref, w2_ref, w3_ref, bias1_ref, bias2_ref,
         )
         loads = [
@@ -58,7 +58,13 @@
         d = lax.axis_index("depth")
         h = lax.axis_index("height")
         v = lax.axis_index("view")
-        z = d * views + v
+
+        def turn(depth, view):
+            return jnp.where(lax.rem(depth, 2) == 1, views - 1 - view, view)
+
+        brick = turn(d, v)
+        moved = brick != v
+        z = d * views + brick
         planes = depths * views
 
         def exists(dz, dy):
@@ -78,7 +84,8 @@
 
         def neighbour(dz, dy):
             to = z + dz
-            return {"depth": lax.div(to, views), "view": lax.rem(to, views), "height": h + dy}
+            row = lax.div(to, views)
+            return {"depth": row, "view": turn(row, lax.rem(to, views)), "height": h + dy}
 
         def halo_slot(index, dz, dy):
             if dy == 0:
@@ -173,17 +180,31 @@
         def part_copy(k):
             to = lax.rem(v + k, views)
             return pltpu.make_async_remote_copy(
-                src_ref=part.at[to], dst_ref=rsbuf.at[k],
+                src_ref=part.at[turn(d, to)], dst_ref=rsbuf.at[k],
                 send_sem=view_send.at[0, k], recv_sem=view_recv.at[0, k],
                 device_id={"view": to}, device_id_type=MESH,
             )
 
         for k in range(1, views):
             part_copy(k).start()
-        loads[4].wait()
-        halo_start(OUTG)
-        for load in loads[5:]:
+        for load in loads[4:]:
             load.wait()
+
+        def swap_copy(n):
+            return pltpu.make_async_remote_copy(
+                src_ref=(outg_ref, field_own)[n],
+                dst_ref=(vol.at[OUTG, 1, pl.ds(1, rows_y)], field_in)[n],
+                send_sem=swap_send.at[n], recv_sem=swap_recv.at[n],
+                device_id={"view": brick}, device_id_type=MESH,
+            )
+
+        @pl.when(moved)
+        def _():
+            swap_copy(0).start()
+
+        @pl.when(jnp.logical_not(moved))
+        def _():
+            vol[OUTG, 1, pl.ds(1, rows_y)] = outg_ref[...]
 
         for n, ref in enumerate((w1_ref, w2_ref, w3_ref)):
             tiles_f = [ref[t].astype(F32) for t in range(27)]
@@ -329,23 +350,29 @@
             for k in range(1, group):
                 ar_b(n, k).wait_send()
 
-        lifted = part[v].astype(F32)
+        lifted = part[brick].astype(F32)
         for k in range(1, views):
             part_copy(k).wait_recv()
             lifted = lifted + rsbuf[k].astype(F32)
         put(LIFT, lifted.astype(BF16))
         halo_start(LIFT)
 
-        halo_wait(OUTG)
-        up_second = conv(3, im2col(OUTG))
-        out_pieces = grad_rows(vol[OUTG, 1, pl.ds(1, rows_y)].reshape(cells, width))
-
+        @pl.when(moved)
+        def _():
+            swap_copy(0).wait_recv()
+
+        halo_start(OUTG)
         halo_wait(LIFT)
-        pre_first = conv(0, im2col(LIFT)) + tall_bias(bias1_ref)
+        columns_first = im2col(LIFT)
+        pre_first = conv(0, columns_first) + tall_bias(bias1_ref)
         act_first = jax.nn.silu(pre_first).astype(BF16)
         put(ACT1, act_first)
         halo_start(ACT1)
         slope_of_first = silu_grad(pre_first)
+
+        halo_wait(OUTG)
+        up_second = conv(3, im2col(OUTG))
+        out_pieces = grad_rows(vol[OUTG, 1, pl.ds(1, rows_y)].reshape(cells, width))
 
         halo_wait(ACT1)
         columns_second = im2col(ACT1)
@@ -373,13 +400,18 @@
         halo_wait(ACT2)
         columns_third = im2col(ACT2)
         field = conv(2, columns_third)
-        field_ref[0] = field.astype(BF16).reshape(rows_y, channels, width)
+        field_own[...] = field.astype(BF16).reshape(rows_y, channels, width)
+
+        @pl.when(moved)
+        def _():
+            swap_copy(1).start()
+
         keep_grad(0, half, weight_grad(columns_third, out_pieces))
         reduce_start(0)
 
         halo_wait(BACK1)
         lift_grad = conv(5, im2col(BACK1)).astype(BF16)
-        grid[v] = lift_grad.reshape(rows_y, channels, width)
+        grid[brick] = lift_grad.reshape(rows_y, channels, width)
 
         def grid_copy(k, place):
             return pltpu.make_async_remote_copy(
@@ -389,11 +421,11 @@
             )
 
         for k in range(1, views):
-            grid_copy(k, v).start()
+            grid_copy(k, brick).start()
         reduce_middle(1)
         reduce_middle(0)
         for k in range(1, views):
-            grid_copy(k, lax.rem(v + views - k, views)).wait_recv()
+            grid_copy(k, turn(d, lax.rem(v + views - k, views))).wait_recv()
         reduce_last(1)
         reduce_last(0)
         camera = jnp.zeros((tiles * channels, width), F32)
@@ -403,13 +435,24 @@
             )
             camera += jnp.dot(picked, foot_ref[k], preferred_element_type=F32)
         camera_ref[...] = camera.reshape(tiles, channels, width)
+        @pl.when(moved)
+        def _():
+            swap_copy(1).wait_recv()
+            field_ref[0] = field_in[...]
+            for n in range(2):
+                swap_copy(n).wait_send()
+
+        @pl.when(jnp.logical_not(moved))
+        def _():
+            field_ref[0] = field_own[...]
+
         reduce_end(1)
         reduce_end(0)
         for index in range(6):
             halo_drain(index)
         for k in range(1, views):
             part_copy(k).wait_send()
-            grid_copy(k, v).wait_send()
+            grid_copy(k, brick).wait_send()
         for n in range(2):
             reduce_drain(n)
 
@@ -437,6 +480,11 @@
             pltpu.VMEM((1, channels), F32),
             pltpu.VMEM((1, channels), F32),
             pltpu.SemaphoreType.DMA((10,)),
+            pltpu.VMEM(plane, BF16),
+            pltpu.VMEM(plane, BF16),
+            pltpu.VMEM(plane, BF16),
+            pltpu.SemaphoreType.DMA((2,)),
+            pltpu.SemaphoreType.DMA((2,)),
             pltpu.VMEM((6, srows, wrows), BF16),
             pltpu.VMEM((6, 3, rows_y + 2, channels, width), BF16),
             pltpu.VMEM((views,) + plane, BF16),

time: 41.4 us -> 39.4 us (0.952)
  Pallas kernels: 40.6 us -> 38.6 us
    pallas_call x1, Pallas kernels: 38.6 us -> 36.6 us  [body(): call(tile_bricks, tile_rows, camera_feats, footprint_slot_weights, tap_ti...]
where the time goes in v3:
time: 39.4 us; the launch traced here: 39.2 us
  Pallas kernels  38.6 us (98%)
  between operations  0.64 us (2%)
    pallas_call x1, Pallas kernels, body(): call(tile_bricks, tile_rows, camera_feats, footprint_slot_weights, tap_ti...  36.6 us
    pallas_call x1, Pallas kernels, finish(): pl.pallas_call(kernel, out_shape=(jax.ShapeDtypeStruct(field.shape, field...  2 us

profile of v3, /device:TPU:0, one launch (start us, length us, event | category | flops | bytes accessed | tf_op | source)
XLA Modules:
  0.0 39.2 jit_solution(14452936921579558962)
XLA Ops:
  0.6 36.6 %shard_map.129 = (bf16[1,8,16,128]{3,2,1,0:T(8,128)(2,1)}, f32[8,16,128]{2,1,0:T(8,128)}, f32[192,128]{1,0:T(8,128)}, f32[128,128]{1,0:T(8,128)}) custom-call(s32[8,8]{1,0:T(8,128)} %bricks_hbm.1, s32[8,8]{1,0:T(8,128)} %rows_hbm.1, bf16[8,16,128]{2,1,0:T(8,128)(2,1)} %feats_hbm.1, bf16[8,128,128]{2,1,0:T(8,128)(2,1)} %foot_hbm.1, ...), custom_call_target="tpu_custom_call" | custom-call | tf_op jit(solution)/shard_map/pallas_call | solution.py:565
  37.2 2.0 %shard_map.130 = (bf16[1,8,16,128]{3,2,1,0:T(8,128)(2,1)}, f32[8,16,128]{2,1,0:T(8,128)}, f32[3,27,16,16]{3,2,1,0:T(8,128)}, f32[2,16]{1,0:T(2,128)}) custom-call(bf16[1,8,16,128]{3,2,1,0:T(8,128)(2,1)} %get-tuple-element.12.field_in, f32[8,16,128]{2,1,0:T(8,128)} %get-tuple-element.13.camera_in, f32[192,128]{1,0:T(8,128)} %get-tuple-element.14.early_ref, ...), custom_call_target="tpu_custom_call" | custom-call | tf_op jit(solution)/shard_map/pallas_call | solution.py:529
